TPU v7x, 64 devices: a 2x2x8 block of a 4x4x8 slice. The times are simulated.
64 devices in a mesh: dp: 8 (over x, y, core), tp: 8 (over z).
Axes of the slice: x: 2, y: 2, z: 8, core: 2. Of those that a mesh axis runs over, the one named last changes fastest.
The devices are a block of a 4x4x8 slice.
Arguments:
- x: bfloat16 [512, 8192], P('dp'), parts along dimension 0
- k_cache: bfloat16 [512, 2048, 8, 128], P('dp', None, 'tp'), parts along dimension 0
- v_cache: bfloat16 [512, 2048, 8, 128], P('dp', None, 'tp'), parts along dimension 0
- gain_a: bfloat16 [8192], replicated
- wq: bfloat16 [8192, 8192], P(None, 'tp')
- wo: bfloat16 [8192, 8192], P('tp')
- gain_m: bfloat16 [8192], replicated
- w_gate: bfloat16 [8192, 28672], P(None, 'tp')
- w_up: bfloat16 [8192, 28672], P(None, 'tp')
- w_down: bfloat16 [28672, 8192], P('tp')
Outputs:
- output: bfloat16 [512, 8192], P('dp'), parts along dimension 0
There are 8 independent parts. A program takes and returns all parts, laid end to end along the dimension named above; an argument that names none is the same for every part.
All inputs are finite; a program needn't handle non-finite values.
Results may differ from a plain program's by a relative error of at most 0.017.
Values are sent between devices in bfloat16 or wider.
A program may use at most 768 MiB of HBM per device.

v0:
```python
import jax
import jax.numpy as jnp
from jax import lax
from jax.sharding import PartitionSpec as P

HEAD = 128
THETA = 10000


def normed(x, gain):
    wide = x.astype(jnp.float32)
    scale = lax.rsqrt(jnp.mean(wide * wide, -1, keepdims=True) + 1e-6)
    return (wide * scale * gain.astype(jnp.float32)).astype(jnp.bfloat16)


def turned(t, place, theta):
    half = t.shape[-1] // 2
    angle = place.astype(jnp.float32)[:, None] * theta ** (-jnp.arange(half, dtype=jnp.float32) / half)
    cos, sin = jnp.cos(angle)[:, None], jnp.sin(angle)[:, None]
    a, b = t[..., :half].astype(jnp.float32), t[..., half:].astype(jnp.float32)
    return jnp.concatenate([a * cos - b * sin, b * cos + a * sin], -1).astype(jnp.bfloat16)


def matmul(a, w):
    return jnp.dot(a, w, preferred_element_type=jnp.float32).astype(jnp.bfloat16)


def einsum(form, a, b):
    return jnp.einsum(form, a.astype(jnp.float32), b.astype(jnp.float32))


def seen_by(a, wq, k_cache, v_cache, head, theta):
    batch, cache, kv_heads = k_cache.shape[:3]
    place = jnp.full((batch,), cache - 1)
    q = turned(matmul(a, wq).reshape(batch, -1, head), place, theta).reshape(batch, kv_heads, -1, head)
    scores = einsum("bgsd,bugd->bgsu", q, k_cache) * head**-0.5
    weights = jax.nn.softmax(scores, -1).astype(jnp.bfloat16)
    return einsum("bgsu,bugd->bgsd", weights, v_cache).astype(jnp.bfloat16).reshape(batch, -1)


def hidden_of(b, w_gate, w_up):
    gate = jnp.dot(b, w_gate, preferred_element_type=jnp.float32)
    up = jnp.dot(b, w_up, preferred_element_type=jnp.float32)
    return (jax.nn.silu(gate) * up).astype(jnp.bfloat16)


def solution(mesh):
    def added(t, term):
        return (t.astype(jnp.float32) + lax.psum(term.astype(jnp.bfloat16), "tp").astype(jnp.float32)).astype(jnp.bfloat16)

    def step(x, k_cache, v_cache, gain_a, wq, wo, gain_m, w_gate, w_up, w_down):
        seen = seen_by(normed(x, gain_a), wq, k_cache, v_cache, HEAD, THETA)
        h = added(x, jnp.dot(seen, wo, preferred_element_type=jnp.float32))
        return added(h, jnp.dot(hidden_of(normed(h, gain_m), w_gate, w_up), w_down, preferred_element_type=jnp.float32))

    states, cache, columns, rows_of = P("dp", None), P("dp", None, "tp", None), P(None, "tp"), P("tp", None)
    return jax.shard_map(
        step,
        mesh=mesh,
        in_specs=(states, cache, cache, P(None), columns, rows_of, P(None), columns, columns, rows_of),
        out_specs=states,
        check_vma=False,
    )
```

profile of v0, /device:TPU:30, one launch (start us, length us, event | category | flops | bytes accessed | tf_op | source)
XLA Modules:
  0.0 274.0 jit_solution(11168773778337925765)
XLA Ops:
  6.5 0.0 all-reduce.3.cloned.1.call-start
  6.6 0.7 convert_element_type.66
  7.3 1.5 fusion.7
  8.9 9.2 %fusion.20 = bf16[8,8,8,128]{3,1,2,0:T(8,128)(2,1)S(1)} fusion(bf16[8192,1024]{1,0:T(8,128)(2,1)} %param.14, bf16[64,8192]{1,0:T(8,128)(2,1)} %param.10, f32[8192]{0:T(1024)S(1)} %convert_element_type.66, f32[64]{0:T(128)S(1)} %add_rsqrt_fusion.1), kind=kOutput, calls=%fused_computation.31 | convolution fusion | flops 1075904512 | bytes 17989888 | tf_op jit(solution)/shard_map/dot_general | solution.py:25
  18.1 0.1 fusion.35
  18.3 16.9 %fusion.49 = (f32[64,8]{1,0:T(8,128)S(1)}, f32[64,8,2048]{2,1,0:T(8,128)}) fusion(bf16[64,2048,1,128]{3,1,2,0:T(8,128)(2,1)} %param.11, bf16[64,8,64]{2,1,0:T(8,128)(2,1)S(1)} %get-tuple-element.8, bf16[64,8,64]{2,1,0:T(8,128)(2,1)S(1)} %get-tuple-element.7), kind=kOutput, calls=%fused_computation.62 | convolution fusion | flops 271845376 | bytes 37881856 | tf_op jit(solution)/shard_map/sub | solution.py:37
  35.2 14.1 %fusion.17 = bf16[64,8,128]{2,1,0:T(8,128)(2,1)S(1)} fusion(bf16[64,2048,1,128]{3,1,2,0:T(8,128)(2,1)} %param.12, f32[64,8,2048]{2,1,0:T(8,128)} %get-tuple-element.10, f32[64,8]{1,0:T(8,128)S(1)} %get-tuple-element.9), kind=kOutput, calls=%fused_computation.29 | convolution fusion | flops 270598144 | bytes 37881856 | tf_op jit(solution)/shard_map/bgsu,bugd->bgsd/dot_general | solution.py:29
  49.3 0.0 copy-start.1
  49.3 0.0 copy-start
  49.4 9.9 %convolution_convert_fusion.1 = bf16[64,8192]{1,0:T(8,128)(2,1)} fusion(bf16[1024,8192]{1,0:T(8,128)(2,1)} %param.15, bf16[8,8,8,128]{3,2,1,0:T(8,128)(2,1)S(1)} %bitcast.28), kind=kOutput, calls=%fused_computation.6 | convolution fusion | flops 1074266112 | bytes 17956864 | tf_op jit(solution)/shard_map/dot_general | solution.py:53
  59.2 0.1 all-reduce.3.cloned.1.call-update
  59.3 0.2 all-reduce.5.cloned.1.call-start
  59.5 0.0 copy-done.1
  59.5 72.9 %all-reduce.3.cloned.1.call-done = bf16[64,8192]{1,0:T(8,128)(2,1)} async-done(((bf16[64,8192]{1,0:T(8,128)(2,1)}), bf16[64,8192]{1,0:T(8,128)(2,1)}) %all-reduce.3.cloned.1.call-update) | async-done | bytes 1048592 | tf_op jit(solution)/shard_map/psum | solution.py:49
  132.4 0.0 copy-done
  132.4 1.7 fusion.11
  134.2 20.7 %fusion.32 = f32[64,3584]{1,0:T(8,128)S(1)} fusion(bf16[8192,3584]{1,0:T(8,128)(2,1)} %param.17, bf16[64,8192]{1,0:T(8,128)(2,1)S(1)} %get-tuple-element.6, f32[8192]{0:T(1024)S(1)} %convert_element_type.77, f32[64]{0:T(128)S(1)} %add_rsqrt_fusion), kind=kOutput, calls=%fused_computation.44 | convolution fusion | flops 3760193536 | bytes 60719360 | tf_op jit(solution)/shard_map/dot_general | solution.py:42
  154.9 42.0 %convolution_convert_fusion = bf16[64,8192]{1,0:T(8,128)(2,1)} fusion(bf16[3584,8192]{1,0:T(8,128)(2,1)} %param.19, bf16[8192,3584]{1,0:T(8,128)(2,1)} %param.18, f32[64,3584]{1,0:T(8,128)S(1)} %fusion.32, bf16[64,8192]{1,0:T(8,128)(2,1)S(1)} %get-tuple-element.6, f32[8192]{0:T(1024)S(1)} %convert_element_type.77, f32[64]{0:T(128)S(1)} %add_rsqrt_fusion), kind=kOutput, calls=%fused_computation.5 | convolution fusion | flops 7520190464 | bytes 120488192 | tf_op jit(solution)/shard_map/dot_general | solution.py:54
  196.9 0.1 all-reduce.5.cloned.1.call-update
  197.0 67.8 %all-reduce.5.cloned.1.call-done = bf16[64,8192]{1,0:T(8,128)(2,1)} async-done(((bf16[64,8192]{1,0:T(8,128)(2,1)}), bf16[64,8192]{1,0:T(8,128)(2,1)}) %all-reduce.5.cloned.1.call-update) | async-done | bytes 1048592 | tf_op jit(solution)/shard_map/psum | solution.py:49
  264.7 2.4 fusion.14
  (5 shorter events, 0.1 us)
Async XLA Ops:
  6.5 125.9 %all-reduce.3.cloned.1.call-start = ((), (), s32[]{:S(2)}) async-start(), calls=%async_computation | async-start | bytes 2097152 | tf_op jit(solution)/shard_map/psum | solution.py:49
  49.3 10.2 %copy-start.1 = (bf16[8192]{0:T(1024)(128)(2,1)S(1)}, bf16[8192]{0:T(1024)(128)(2,1)}, u32[]{:S(2)}) copy-start(bf16[8192]{0:T(1024)(128)(2,1)} %param.16) | copy-start | bytes 49156
  49.3 83.1 %copy-start = (bf16[64,8192]{1,0:T(8,128)(2,1)S(1)}, bf16[64,8192]{1,0:T(8,128)(2,1)}, u32[]{:S(2)}) copy-start(bf16[64,8192]{1,0:T(8,128)(2,1)} %param.10) | copy-start | bytes 3145732
  59.3 205.5 %all-reduce.5.cloned.1.call-start = ((), (), s32[]{:S(2)}) async-start(), calls=%async_computation.1 | async-start | bytes 2097152 | tf_op jit(solution)/shard_map/psum | solution.py:49
Sparse Core Ops, SparseCore 0:
  59.4 73.0 all-reduce.2
  197.1 67.5 all-reduce.4
where the time goes:
time: 275 us; the launch traced here: 274 us
  waiting for transfers between devices  141 us (51%)
  matrix products  113 us (41%)
  between operations  13.5 us (5%)
  other arithmetic  6.58 us (2%)
    psum x2, waiting for transfers between devices, added(): lax.psum(term.astype(jnp.bfloat16), 'tp').astype(jnp.float32)  141 us
    dot_general x1, matrix products, step(): jnp.dot(hidden_of(normed(h, gain_m), w_gate, w_up), w_down, preferred_ele...  42 us
    dot_general x1, matrix products, hidden_of(): gate = jnp.dot(b, w_gate, preferred_element_type=jnp.float32)  20.7 us
    sub x1, matrix products, seen_by(): weights = jax.nn.softmax(scores, -1).astype(jnp.bfloat16)  16.9 us
    dot_general x1, matrix products, einsum(): return jnp.einsum(form, a.astype(jnp.float32), b.astype(jnp.float32))  14.1 us
    dot_general x1, matrix products, step(): h = added(x, jnp.dot(seen, wo, preferred_element_type=jnp.float32))  9.85 us
    dot_general x1, matrix products, matmul(): jnp.dot(a, w, preferred_element_type=jnp.float32).astype(jnp.bfloat16)  9.21 us
  transfers between devices with their start and end apart: 2, of which 2 were waited for; matrix products, arithmetic and copies ran while one was open for 0% of the time, Pallas kernels for 0%

commit v1 on v0

v1 whole, which is shorter than its diff:
```python
import functools

import jax
import jax.numpy as jnp
from jax import lax
from jax.experimental import pallas as pl
from jax.experimental.pallas import tpu as pltpu
from jax.sharding import PartitionSpec as P

HEAD = 128
THETA = 10000
F32, BF16 = jnp.float32, jnp.bfloat16

DEEP, WIDE = 4096, 256
SLOTS = 24
HELD = 8


def mult(v, k):
    return pl.multiple_of(v, k)


def layer(n, x_hbm, kc, vc, gain_a, wq, wo, gain_m, wg, wu, wd, cos, sin, out,
          ring, x, ab, states, part, hidden, q3, seen3, far1, near1, far2, near2, sf1, sn1, sf2, sn2,
          slot_sem, x_sem, send1, send2, rf1, rn1, rf2, rn2, gf1, gn1, gf2, gn2):
    me = lax.axis_index("tp")
    rows, d = x_hbm.shape
    head = kc.shape[2]
    keys = kc.shape[1]
    half = n // 2
    up_blocks = wg.shape[1] // WIDE
    down_rows = wd.shape[0]
    down_blocks = d // WIDE
    mlp = 4 * up_blocks + down_blocks
    chunk_rows = 16
    chunks = rows // chunk_rows

    def put(src, dst, slot):
        pltpu.make_async_copy(src, dst, slot_sem.at[slot]).start()

    def ready(slot, deep=DEEP):
        pltpu.make_async_copy(wg.at[pl.ds(0, deep), pl.ds(0, WIDE)], ring.at[slot, pl.ds(0, deep)], slot_sem.at[slot]).wait()

    def start_wq(cb, part_):
        slot = 2 * cb + part_
        put(wq.at[pl.ds(part_ * DEEP, DEEP), pl.ds(mult(cb * WIDE, WIDE), WIDE)], ring.at[slot], slot)

    def start_wo(cb):
        slot = HELD + cb
        for j in range(4):
            put(wo.at[:, pl.ds(mult(cb * 4 * WIDE + j * WIDE, WIDE), WIDE)], ring.at[slot, pl.ds(j * 1024, 1024)], slot)

    def kv_slot(j):
        return lax.rem(2 * HELD + lax.rem(j, SLOTS - HELD), SLOTS)

    def start_kv(it):
        for which, src in enumerate((kc, vc)):
            slot = kv_slot(2 * it + which)
            for p in range(2):
                for side in range(2):
                    put(src.at[it * 4 + 2 * p + side], ring.at[slot, pl.ds(p * keys, keys), pl.ds(side * head, head)], slot)

    def mlp_slot(m):
        return lax.rem(2 * HELD + m, SLOTS)

    def start_mlp4(m):
        @pl.when(m < 4 * up_blocks)
        def _():
            col = pl.ds(mult(m // 4 * WIDE, WIDE), WIDE)
            for r in range(4):
                slot = mlp_slot(m + r)
                put((wg, wu)[r // 2].at[pl.ds(r % 2 * DEEP, DEEP), col], ring.at[slot], slot)

        @pl.when((m >= 4 * up_blocks) & (m < mlp))
        def _():
            for r in range(4):
                slot = mlp_slot(m + r)
                nb = m + r - 4 * up_blocks
                put(wd.at[:, pl.ds(mult(nb * WIDE, WIDE), WIDE)], ring.at[slot, pl.ds(0, down_rows)], slot)

    x_copy = pltpu.make_async_copy(x_hbm, x, x_sem)
    x_copy.start()
    for cb in range(4):
        for part_ in range(2):
            start_wq(cb, part_)
    for it in range(4):
        start_kv(it)
    barrier = pltpu.get_barrier_semaphore()
    for step in (1, n - 1):
        pl.semaphore_signal(barrier, inc=1, device_id={"tp": lax.rem(me + step, n)}, device_id_type=pl.DeviceIdType.MESH)

    def steps(s, g, piece_rows, far, near, sf, sn, send, rf, rn, gf, gn, whole, residual, done):
        sign = 1 - 2 * lax.rem(g, 2)
        to_far = lax.rem(me + sign + n, n)
        to_near = lax.rem(me - sign + n, n)

        def owner(k):
            return lax.rem(me + k * sign + 2 * n, n)

        def at(o):
            return pl.ds(mult((g * n + o) * piece_rows, piece_rows), piece_rows)

        def remote(src, dst, i, sem, to):
            return pltpu.make_async_remote_copy(src_ref=src, dst_ref=dst, send_sem=send.at[i], recv_sem=sem,
                                                device_id={"tp": to}, device_id_type=pl.DeviceIdType.MESH)

        def far_copy(k):
            return remote(sf.at[k], far.at[g, k], k, rf.at[g, k], to_far)

        def near_copy(k):
            return remote(sn.at[k], near.at[g, k], half + k, rn.at[g, k], to_near)

        def far_out(k):
            piece = whole.at[at(owner(-k))]
            return remote(piece, piece, 2 * half - 1 + k, gf.at[g, k], to_far)

        def near_out(k):
            piece = whole.at[at(owner(k))]
            return remote(piece, piece, 3 * half - 1 + k, gn.at[g, k], to_near)

        def far_in(k):
            piece = whole.at[at(owner(-k - 1))]
            return remote(piece, piece, 2 * half - 1 + k, gf.at[g, k], to_far)

        def near_in(k):
            piece = whole.at[at(owner(k + 1))]
            return remote(piece, piece, 3 * half - 1 + k, gn.at[g, k], to_near)

        def free(copy):
            @pl.when(g > 0)
            def _():
                copy.wait_send()

        if s == "drain":
            for k in range(half):
                far_copy(k).wait_send()
                far_out(k).wait_send()
            for k in range(half - 1):
                near_copy(k).wait_send()
                near_out(k).wait_send()
            return
        if s < half:
            value = part[at(owner(half - s)), :]
            if s > 0:
                far_copy(s - 1).wait_recv()
                value = value + far[g, s - 1].astype(F32)
            free(far_copy(s))
            sf[s] = value.astype(BF16)
            far_copy(s).start()
        if 1 <= s < half:
            value = part[at(owner(s - half)), :]
            if s > 1:
                near_copy(s - 2).wait_recv()
                value = value + near[g, s - 2].astype(F32)
            free(near_copy(s - 1))
            sn[s - 1] = value.astype(BF16)
            near_copy(s - 1).start()
        if s == half:
            far_copy(half - 1).wait_recv()
            near_copy(half - 2).wait_recv()
            value = part[at(me), :] + far[g, half - 1].astype(F32) + near[g, half - 2].astype(F32)
            whole[at(me), :] = (residual(g) + value).astype(BF16)
            free(far_out(0))
            far_out(0).start()
            free(near_out(0))
            near_out(0).start()
        if half < s <= 2 * half:
            k = s - half - 1
            far_in(k).wait_recv()
            if k + 1 < half:
                free(far_out(k + 1))
                far_out(k + 1).start()
            if k < half - 1:
                near_in(k).wait_recv()
                if k + 1 < half - 1:
                    free(near_out(k + 1))
                    near_out(k + 1).start()
            if s == 2 * half:
                done(g)

    blocks = d // 128

    def norm_x(i, _):
        r = pl.ds(mult(i * 16, 16), 16)
        total = jnp.zeros((16, 128), F32)
        for k in range(blocks):
            wide = x[r, pl.ds(k * 128, 128)].astype(F32)
            total = total + wide * wide
        scale = lax.rsqrt(jnp.sum(total, -1, keepdims=True) * (1.0 / d) + 1e-6)
        for k in range(blocks):
            c = pl.ds(k * 128, 128)
            ab[r, c] = (x[r, c].astype(F32) * scale * gain_a[:, c]).astype(BF16)
        return 0

    x_copy.wait()
    lax.fori_loop(0, rows // 16, norm_x, 0)

    def project(cb, _):
        ready(2 * cb)
        acc = jnp.dot(ab[:, pl.ds(0, DEEP)], ring[2 * cb], preferred_element_type=F32)
        ready(2 * cb + 1)
        acc = acc + jnp.dot(ab[:, pl.ds(DEEP, DEEP)], ring[2 * cb + 1], preferred_element_type=F32)
        for j in range(2):
            t = acc[:, j * head:(j + 1) * head].astype(BF16).astype(F32)
            t = t * cos[...] + pltpu.roll(t, head // 2, 1) * sin[...]
            q3[pl.ds(2 * cb + j, rows, stride=8), :] = t.astype(BF16).astype(F32)
        start_kv(4 + cb)
        start_wo(2 * cb)
        start_wo(2 * cb + 1)
        return 0

    lax.fori_loop(0, 4, project, 0)
    pl.semaphore_wait(barrier, 2)

    def residual1(g):
        r = pl.ds(mult(g * chunk_rows, chunk_rows), chunk_rows)
        cols = [x[r, pl.ds(mult(me * 1024 + k * 128, 128), 128)].astype(F32) for k in range(8)]
        return jnp.concatenate(cols, 0)

    def done1(g):
        total = jnp.zeros((chunk_rows, 128), F32)
        for k in range(blocks):
            wide = states[pl.ds(mult(g * 1024 + k * 16, 16), 16), :].astype(F32)
            total = total + wide * wide
        scale = lax.rsqrt(jnp.sum(total, -1, keepdims=True) * (1.0 / d) + 1e-6)
        r = pl.ds(mult(g * chunk_rows, chunk_rows), chunk_rows)
        for k in range(blocks):
            c = pl.ds(k * 128, 128)
            wide = states[pl.ds(mult(g * 1024 + k * 16, 16), 16), :].astype(F32)
            ab[r, c] = (wide * scale * gain_m[:, c]).astype(BF16)

    first = functools.partial(steps, piece_rows=chunk_rows * 8, far=far1, near=near1, sf=sf1, sn=sn1,
                              send=send1, rf=rf1, rn=rn1, gf=gf1, gn=gn1, whole=states, residual=residual1, done=done1)

    def tick1(t):
        for s in range(2 * half, -1, -1):
            @pl.when((lax.rem(t - s + 16, 2) == 0) & (t >= s) & (t - s < 2 * chunks))
            def _():
                first(s, (t - s) // 2)

    def attend(it):
        ks, vs = kv_slot(2 * it), kv_slot(2 * it + 1)
        ready(ks)
        zero = jnp.zeros((8, head), F32)
        weights = []
        for p in range(2):
            s0 = (it * 4 + 2 * p) * 8
            q = jnp.concatenate([jnp.concatenate([q3[pl.ds(mult(s0, 8), 8), :], zero], 1),
                                 jnp.concatenate([zero, q3[pl.ds(mult(s0 + 8, 8), 8), :]], 1)], 0).astype(BF16)
            scores = lax.dot_general(q, ring[ks, pl.ds(p * keys, keys)], (((1,), (1,)), ((), ())),
                                     preferred_element_type=F32) * head**-0.5
            e = jnp.exp(scores - jnp.max(scores, -1, keepdims=True))
            weights.append((e * (1.0 / jnp.sum(e, -1, keepdims=True))).astype(BF16))
        ready(vs)
        for p in range(2):
            s0 = (it * 4 + 2 * p) * 8
            o = jnp.dot(weights[p], ring[vs, pl.ds(p * keys, keys)], preferred_element_type=F32)
            o = o.astype(BF16).astype(F32)
            seen3[pl.ds(mult(s0, 8), 8), :] = o[:8, :head]
            seen3[pl.ds(mult(s0 + 8, 8), 8), :] = o[8:, head:]

        @pl.when(it < 8)
        def _():
            start_kv(it + 8)

    def rows_chunk(c, _):
        def four(i, _):
            it = c * 4 + i
            attend(it)

            @pl.when((lax.rem(it, 2) == 1) & (it >= 8))
            def _():
                start_mlp4(2 * (it - 1 - 8))

            @pl.when(i == 1)
            def _():
                tick1(2 * c - 1)
            return 0

        lax.fori_loop(0, 4, four, 0)
        seen = jnp.concatenate([seen3[pl.ds(c * 128 + h, chunk_rows, stride=8), :] for h in range(8)], 1).astype(BF16)

        def columns(cb, _):
            @pl.when(c == 0)
            def _():
                ready(HELD + cb)
            for j in range(4):
                acc = jnp.dot(seen, ring[HELD + cb, pl.ds(j * 1024, 1024)], preferred_element_type=F32)
                base = (c * 8 + cb) * 128 + j * 32
                part[pl.ds(mult(base, 16), 16), :] = acc[:, :128]
                part[pl.ds(mult(base + 16, 16), 16), :] = acc[:, 128:]
            return 0

        lax.fori_loop(0, 8, columns, 0)
        tick1(2 * c)
        return 0

    lax.fori_loop(0, chunks, rows_chunk, 0)
    start_mlp4(16)
    start_mlp4(20)

    def rest1(t, _):
        tick1(t)
        return 0

    lax.fori_loop(2 * chunks - 1, 2 * (chunks - 1) + 2 * half + 1, rest1, 0)

    def gate_up(cb, _):
        m = 4 * cb
        outs = []
        for r in range(2):
            s0, s1 = mlp_slot(m + 2 * r), mlp_slot(m + 2 * r + 1)
            ready(s0)
            acc = jnp.dot(ab[:, pl.ds(0, DEEP)], ring[s0], preferred_element_type=F32)
            ready(s1)
            outs.append(acc + jnp.dot(ab[:, pl.ds(DEEP, DEEP)], ring[s1], preferred_element_type=F32))
        hidden[:, pl.ds(mult(cb * WIDE, WIDE), WIDE)] = (jax.nn.silu(outs[0]) * outs[1]).astype(BF16)
        start_mlp4(m + SLOTS)
        return 0

    lax.fori_loop(0, up_blocks, gate_up, 0)

    def residual2(g):
        pieces = [states[pl.ds(mult(c * 1024 + g * 128 + me * 16, 16), 16), :] for c in range(chunks)]
        return jnp.concatenate(pieces, 0).astype(F32)

    groups = d // 1024
    second = functools.partial(steps, piece_rows=rows, far=far2, near=near2, sf=sf2, sn=sn2,
                               send=send2, rf=rf2, rn=rn2, gf=gf2, gn=gn2, whole=out, residual=residual2, done=lambda g: None)

    def down(t, _):
        @pl.when(t < groups)
        def _():
            def block(i, _):
                nb = 4 * t + i
                slot = mlp_slot(4 * up_blocks + nb)
                ready(slot, down_rows)
                acc = jnp.dot(hidden[...], ring[slot, pl.ds(0, down_rows)], preferred_element_type=F32)
                part[pl.ds(mult(nb * 2 * rows, rows), rows), :] = acc[:, :128]
                part[pl.ds(mult(nb * 2 * rows + rows, rows), rows), :] = acc[:, 128:]
                return 0

            lax.fori_loop(0, 4, block, 0)
            start_mlp4(4 * up_blocks + 4 * t + SLOTS)

        for s in [0] + list(range(2 * half, 0, -1)):
            @pl.when((t >= s) & (t - s < groups))
            def _():
                second(s, t - s)
        return 0

    lax.fori_loop(0, groups + 2 * half, down, 0)
    first("drain", jnp.int32(chunks - 1))
    second("drain", jnp.int32(groups - 1))


def solution(mesh):
    n = mesh.shape["tp"]

    def step(x, k_cache, v_cache, gain_a, wq, wo, gain_m, w_gate, w_up, w_down):
        rows, d = x.shape
        batch, keys, _, head = k_cache.shape
        ff = w_gate.shape[1]
        place = jnp.full((1,), keys - 1)
        half = head // 2
        angle = place.astype(F32)[:, None] * THETA ** (-jnp.arange(half, dtype=F32) / half)
        cos, sin = jnp.cos(angle), jnp.sin(angle)
        cos = jnp.concatenate([cos, cos], -1)
        sin = jnp.concatenate([-sin, sin], -1)
        any_, vmem = pl.BlockSpec(memory_space=pl.ANY), pl.BlockSpec(memory_space=pltpu.VMEM)
        far, near = n // 2, n // 2 - 1
        chunks, groups = rows // 16, d // 1024
        dma = pltpu.SemaphoreType.DMA
        out = pl.pallas_call(
            functools.partial(layer, n),
            out_shape=jax.ShapeDtypeStruct((rows * d // 128, 128), BF16),
            in_specs=[any_, any_, any_, vmem, any_, any_, vmem, any_, any_, any_, vmem, vmem],
            out_specs=vmem,
            scratch_shapes=[
                pltpu.VMEM((SLOTS, DEEP, WIDE), BF16),
                pltpu.VMEM((rows, d), BF16),
                pltpu.VMEM((rows, d), BF16),
                pltpu.VMEM((rows * d // 128, 128), BF16),
                pltpu.VMEM((rows * d // 128, 128), F32),
                pltpu.VMEM((rows, ff), BF16),
                pltpu.VMEM((rows * 8, head), F32),
                pltpu.VMEM((rows * 8, head), F32),
                pltpu.VMEM((chunks, far, 128, 128), BF16),
                pltpu.VMEM((chunks, near, 128, 128), BF16),
                pltpu.VMEM((groups, far, rows, 128), BF16),
                pltpu.VMEM((groups, near, rows, 128), BF16),
                pltpu.VMEM((far, 128, 128), BF16),
                pltpu.VMEM((near, 128, 128), BF16),
                pltpu.VMEM((far, rows, 128), BF16),
                pltpu.VMEM((near, rows, 128), BF16),
                dma((SLOTS,)),
                dma(()),
                dma((2 * (far + near),)),
                dma((2 * (far + near),)),
                dma((chunks, far)), dma((chunks, near)),
                dma((groups, far)), dma((groups, near)),
                dma((chunks, far)), dma((chunks, near)),
                dma((groups, far)), dma((groups, near)),
            ],
            compiler_params=pltpu.CompilerParams(collective_id=0, has_side_effects=True, vmem_limit_bytes=67043328),
            name="decoder_layer",
        )(x, k_cache.reshape(batch, keys, head), v_cache.reshape(batch, keys, head), gain_a.astype(F32)[None], wq, wo,
          gain_m.astype(F32)[None], w_gate, w_up, w_down, cos, sin)
        return out.reshape(d // 128, rows, 128).transpose(1, 0, 2).reshape(rows, d)

    states, cache, columns, rows_of = P("dp", None), P("dp", None, "tp", None), P(None, "tp"), P("tp", None)
    return jax.shard_map(
        step,
        mesh=mesh,
        in_specs=(states, cache, cache, P(None), columns, rows_of, P(None), columns, columns, rows_of),
        out_specs=states,
        check_vma=False,
    )
```

time: 275 us -> 191 us (0.69)
  Pallas kernels: 0 us -> 184 us
  waiting for transfers between devices: 141 us -> 0 us
  matrix products: 113 us -> 0 us
  between operations: 13.5 us -> 0.02 us
    pallas_call x0 -> x1, Pallas kernels: none -> 184 us  [step(): pl.pallas_call(functools.partial(layer, n), out_shape=jax.ShapeDtypeStruc...]
    psum x2 -> x0, waiting for transfers between devices: 141 us -> none  [added(): lax.psum(term.astype(jnp.bfloat16), 'tp').astype(jnp.float32)]
    dot_general x5 -> x0, matrix products: 96 us -> none  [the longest x1 42 us: step(): jnp.dot(hidden_of(normed(h, gain_m), w_gate, w_up), w_down, preferred_ele...]
    sub x1 -> x0, matrix products: 16.9 us -> none  [seen_by(): weights = jax.nn.softmax(scores, -1).astype(jnp.bfloat16)]
    reduce_sum x2 -> x0, other arithmetic: 3.22 us -> none  [normed(): scale = lax.rsqrt(jnp.mean(wide * wide, -1, keepdims=True) + 1e-06)]
    convert_element_type x3 -> x0, other arithmetic: 3.16 us -> none  [the longest x1 2.43 us: added(): (t.astype(jnp.float32) + lax.psum(term.astype(jnp.bfloat16), 'tp').astype...]
  transfers between devices with their start and end apart: 2 -> 0, of which waited for: 2 -> 0; matrix products, arithmetic and copies ran while one was open for 0% -> 0% of each run, Pallas kernels for 0% -> 0%
where the time goes in v1:
time: 191 us
  Pallas kernels  184 us (96%)
  other arithmetic  3.99 us (2%)
  local copies, waits for them, and re-layouts  2.39 us (1%)
    pallas_call x1, Pallas kernels, step(): pl.pallas_call(functools.partial(layer, n), out_shape=jax.ShapeDtypeStruc...  184 us

profile of v1, /device:TPU:30, one launch (start us, length us, event | category | flops | bytes accessed | tf_op | source)
XLA Modules:
  0.0 190.7 jit_solution(15888945491206715845)
XLA Ops:
  0.0 0.1 fusion.1
  0.1 0.7 pad_maximum_fusion.cos
  0.7 0.1 fusion
  0.8 0.6 pad_maximum_fusion.1.sin
  1.3 1.3 broadcast_in_dim.15
  2.7 1.3 broadcast_in_dim.16
  4.0 184.3 %decoder_layer.1 = bf16[4096,128]{1,0:T(8,128)(2,1)} custom-call(bf16[64,8192]{1,0:T(8,128)(2,1)} %x_hbm.1, bf16[64,2048,128]{2,1,0:T(8,128)(2,1)} %bitcast.11, bf16[64,2048,128]{2,1,0:T(8,128)(2,1)} %bitcast.12, f32[1,8192]{1,0:T(1,128)} %bitcast.14, bf16[8192,1024]{1,0:T(8,128)(2,1)} %wq.1, bf16[1024,8192]{1,0:T(8,128)(2,1)} %wo.1, f32[1,8192]{1,0:T(1,128)} %bitcast.15, ...), custom_call_target="tpu_custom_call" | custom-call | tf_op jit(solution)/shard_map/decoder_layer/pallas_call | solution.py:374
  188.3 2.4 %copy.14 = bf16[64,8,8,128]{3,2,0,1:T(8,128)(2,1)} copy(bf16[64,8,8,128]{3,2,1,0:T(8,128)(2,1)} %bitcast.13) | data formatting | bytes 2097152 | tf_op jit(solution)/shard_map/reshape | solution.py:409

commit v2 on v1

v2 whole, which is shorter than its diff:
```python
import functools

import jax
import jax.numpy as jnp
import numpy as np
from jax import lax
from jax.experimental import pallas as pl
from jax.experimental.pallas import tpu as pltpu
from jax.sharding import PartitionSpec as P

HEAD = 128
THETA = 10000
F32, BF16 = jnp.float32, jnp.bfloat16

DEEP, WIDE = 4096, 256
SLOTS = 24
HELD = 8


def mult(v, k):
    return pl.multiple_of(v, k)


def layer(n, x_hbm, kc, vc, gain_a_hbm, wq, wo, gain_m_hbm, wg, wu, wd, trig_hbm, out,
          ring, x, ab, states, y, part, hidden, q3, seen3, gain_a, gain_m, trig, box1, box2, stage1, stage2,
          slot_sem, x_sem, out_sem, send1, send2, recv1, recv2):
    me = lax.axis_index("tp")
    rows, d = x_hbm.shape
    head = kc.shape[2]
    keys = kc.shape[1]
    up_blocks = wg.shape[1] // WIDE
    down_rows = wd.shape[0]
    down_blocks = d // WIDE
    mlp = 4 * up_blocks + down_blocks
    chunk_rows = 16
    chunks = rows // chunk_rows

    def put(src, dst, slot):
        pltpu.make_async_copy(src, dst, slot_sem.at[slot]).start()

    def ready(slot, deep=DEEP):
        pltpu.make_async_copy(wg.at[pl.ds(0, deep), pl.ds(0, WIDE)], ring.at[slot, pl.ds(0, deep)], slot_sem.at[slot]).wait()

    def start_wq(cb, part_):
        slot = 2 * cb + part_
        put(wq.at[pl.ds(part_ * DEEP, DEEP), pl.ds(mult(cb * WIDE, WIDE), WIDE)], ring.at[slot], slot)

    def start_wo(cb):
        slot = HELD + cb
        for j in range(4):
            put(wo.at[:, pl.ds(mult(cb * 4 * WIDE + j * WIDE, WIDE), WIDE)], ring.at[slot, pl.ds(j * 1024, 1024)], slot)

    def kv_slot(j):
        return lax.rem(2 * HELD + lax.rem(j, SLOTS - HELD), SLOTS)

    def start_kv(it):
        for which, src in enumerate((kc, vc)):
            slot = kv_slot(2 * it + which)
            for p in range(2):
                for side in range(2):
                    put(src.at[it * 4 + 2 * p + side], ring.at[slot, pl.ds(p * keys, keys), pl.ds(side * head, head)], slot)

    def mlp_slot(m):
        return lax.rem(2 * HELD + m, SLOTS)

    def start_mlp4(m):
        @pl.when(m < 4 * up_blocks)
        def _():
            col = pl.ds(mult(m // 4 * WIDE, WIDE), WIDE)
            for r in range(4):
                slot = mlp_slot(m + r)
                put((wg, wu)[r // 2].at[pl.ds(r % 2 * DEEP, DEEP), col], ring.at[slot], slot)

        @pl.when((m >= 4 * up_blocks) & (m < mlp))
        def _():
            for r in range(4):
                slot = mlp_slot(m + r)
                nb = m + r - 4 * up_blocks
                put(wd.at[:, pl.ds(mult(nb * WIDE, WIDE), WIDE)], ring.at[slot, pl.ds(0, down_rows)], slot)

    small = [pltpu.make_async_copy(a, b, x_sem.at[i]) for i, (a, b) in enumerate(
        ((x_hbm, x), (gain_a_hbm, gain_a), (gain_m_hbm, gain_m), (trig_hbm, trig)))]
    for copy in small:
        copy.start()
    for cb in range(2):
        for part_ in range(2):
            start_wq(cb, part_)
    barrier = pltpu.get_barrier_semaphore()
    for step in (1, 2, n - 2, n - 1):
        pl.semaphore_signal(barrier, inc=1, device_id={"tp": lax.rem(me + step, n)}, device_id_type=pl.DeviceIdType.MESH)

    def steps(s, g, piece_rows, box, stage, send, recv, whole, residual, done):
        sign = 1 - 2 * lax.rem(g + lax.axis_index("dp"), 2)

        def dev(k):
            return lax.rem(me + k * sign + 2 * n, n)

        def at(o):
            return pl.ds(mult((g * n + o) * piece_rows, piece_rows), piece_rows)

        def remote(i, src, dst, to):
            return pltpu.make_async_remote_copy(src_ref=src, dst_ref=dst, send_sem=send.at[i], recv_sem=recv.at[g, i],
                                                device_id={"tp": dev(to)}, device_id_type=pl.DeviceIdType.MESH)

        def term(i, to):
            return remote(i, stage.at[i], box.at[g, i], to)

        def piece(i, owner, to):
            ref = whole.at[at(dev(owner))]
            return remote(7 + i, ref, ref, to)

        def go(copy):
            @pl.when(g > 0)
            def _():
                copy.wait_send()

            copy.start()

        def send_term(i, owner, to, *terms):
            value = part[at(dev(owner)), :]
            for k in terms:
                term(k, 0).wait_recv()
                value = value + box[g, k].astype(F32)
            copy = term(i, to)

            @pl.when(g > 0)
            def _():
                copy.wait_send()

            stage[i] = value.astype(BF16)
            copy.start()

        def forward(k, i, owner, to):
            piece(k, owner, 0).wait_recv()
            go(piece(i, owner, to))

        if s == 0:
            send_term(0, 4, 1)
            send_term(2, -3, -1)
            send_term(1, 1, 1)
        if s == 1:
            send_term(3, 3, 1, 0)
            send_term(4, -2, -1, 2)
        if s == 2:
            send_term(5, 2, 2, 3)
            send_term(6, -1, -1, 4)
        if s == 3:
            value = part[at(me), :]
            for k in (1, 5, 6):
                term(k, 0).wait_recv()
                value = value + box[g, k].astype(F32)
            whole[at(me), :] = (residual(g) + value).astype(BF16)
            for i, to in ((1, 2), (2, -1), (0, 1)):
                go(piece(i, 0, to))
        if s == 4:
            forward(1, 3, -2, 1)
            forward(2, 4, 1, -1)
        if s == 5:
            forward(3, 5, -3, 1)
            forward(4, 6, 2, -1)
        if s == 6:
            for i, owner in ((0, -1), (5, -4), (6, 3)):
                piece(i, owner, 0).wait_recv()
            done(g)
        if s == 7:
            for i in range(7):
                term(i, 1).wait_send()
                piece(i, 0, 1).wait_send()

    LAST = 6

    blocks = d // 128

    def norm_x(i, _):
        r = pl.ds(mult(i * 16, 16), 16)
        total = jnp.zeros((16, 128), F32)
        for k in range(blocks):
            wide = x[r, pl.ds(k * 128, 128)].astype(F32)
            total = total + wide * wide
        scale = lax.rsqrt(jnp.sum(total, -1, keepdims=True) * (1.0 / d) + 1e-6)
        for k in range(blocks):
            c = pl.ds(k * 128, 128)
            ab[r, c] = (x[r, c].astype(F32) * scale * gain_a[k:k + 1, :].astype(F32)).astype(BF16)
        return 0

    for copy in small:
        copy.wait()
    for cb in (2, 3):
        for part_ in range(2):
            start_wq(cb, part_)
    start_kv(0)
    with jax.named_scope("norm"):
        lax.fori_loop(0, rows // 16, norm_x, 0)
    for it in range(1, 4):
        start_kv(it)

    def project(cb, _):
        ready(2 * cb)
        ready(2 * cb + 1)
        acc = jnp.dot(ab[:, pl.ds(0, DEEP)], ring[2 * cb], preferred_element_type=F32)
        acc = acc + jnp.dot(ab[:, pl.ds(DEEP, DEEP)], ring[2 * cb + 1], preferred_element_type=F32)
        for j in range(2):
            t = acc[:, j * head:(j + 1) * head].astype(BF16).astype(F32)
            t = t * trig[0:1, :] + pltpu.roll(t, head // 2, 1) * trig[1:2, :]
            q3[pl.ds(2 * cb + j, rows, stride=8), :] = t.astype(BF16).astype(F32)
        start_kv(4 + cb)
        start_wo(2 * cb)
        start_wo(2 * cb + 1)
        return 0

    with jax.named_scope("project"):
        lax.fori_loop(0, 4, project, 0)
    pl.semaphore_wait(barrier, 4)

    def residual1(g):
        r = pl.ds(mult(g * chunk_rows, chunk_rows), chunk_rows)
        cols = [x[r, pl.ds(mult(me * 1024 + k * 128, 128), 128)].astype(F32) for k in range(8)]
        return jnp.concatenate(cols, 0)

    def done1(g):
        total = jnp.zeros((chunk_rows, 128), F32)
        for k in range(blocks):
            wide = states[pl.ds(mult(g * 1024 + k * 16, 16), 16), :].astype(F32)
            total = total + wide * wide
        scale = lax.rsqrt(jnp.sum(total, -1, keepdims=True) * (1.0 / d) + 1e-6)
        r = pl.ds(mult(g * chunk_rows, chunk_rows), chunk_rows)
        for k in range(blocks):
            c = pl.ds(k * 128, 128)
            wide = states[pl.ds(mult(g * 1024 + k * 16, 16), 16), :].astype(F32)
            ab[r, c] = (wide * scale * gain_m[k:k + 1, :].astype(F32)).astype(BF16)

    first = functools.partial(steps, piece_rows=chunk_rows * 8, box=box1, stage=stage1, send=send1, recv=recv1,
                              whole=states, residual=residual1, done=done1)

    def tick1(t):
        for s in [0] + list(range(1, LAST + 1)):
            since = t - s

            @pl.when((since == 0) | (since == 2) | (since == 4))
            def _():
                with jax.named_scope(f"a{s}"):
                    begin = jnp.where(since == 0, 0, 1 + since // 2)
                    lax.fori_loop(begin, 2 + since // 2, lambda g, _: (first(s, g), 0)[1], 0)

    def attend(it):
        ks, vs = kv_slot(2 * it), kv_slot(2 * it + 1)
        ready(ks)
        ready(vs)
        zero = jnp.zeros((8, head), F32)
        weights = []
        for p in range(2):
            s0 = (it * 4 + 2 * p) * 8
            q = jnp.concatenate([jnp.concatenate([q3[pl.ds(mult(s0, 8), 8), :], zero], 1),
                                 jnp.concatenate([zero, q3[pl.ds(mult(s0 + 8, 8), 8), :]], 1)], 0).astype(BF16)
            scores = lax.dot_general(q, ring[ks, pl.ds(p * keys, keys)], (((1,), (1,)), ((), ())),
                                     preferred_element_type=F32) * head**-0.5
            e = jnp.exp(scores - jnp.max(scores, -1, keepdims=True))
            weights.append((e * (1.0 / jnp.sum(e, -1, keepdims=True))).astype(BF16))
        for p in range(2):
            s0 = (it * 4 + 2 * p) * 8
            o = jnp.dot(weights[p], ring[vs, pl.ds(p * keys, keys)], preferred_element_type=F32)
            o = o.astype(BF16).astype(F32)
            seen3[pl.ds(mult(s0, 8), 8), :] = o[:8, :head]
            seen3[pl.ds(mult(s0 + 8, 8), 8), :] = o[8:, head:]

        @pl.when(it < 8)
        def _():
            start_kv(it + 8)

    def wo_pass(row0, count):
        seen = jnp.concatenate([seen3[pl.ds(row0 * 8 + h, count, stride=8), :] for h in range(8)], 1).astype(BF16)

        def columns(cb2, _):
            for k in range(2):
                @pl.when(row0 == 0)
                def _():
                    ready(HELD + 2 * cb2 + k)

            for k in range(2):
                cb = 2 * cb2 + k
                for j in range(4):
                    acc = jnp.dot(seen, ring[HELD + cb, pl.ds(j * 1024, 1024)], preferred_element_type=F32)
                    for r in range(count // 16):
                        base = ((row0 // 16 + r) * 8 + cb) * 128 + j * 32
                        part[pl.ds(mult(base, 16), 16), :] = acc[r * 16:(r + 1) * 16, :128]
                        part[pl.ds(mult(base + 16, 16), 16), :] = acc[r * 16:(r + 1) * 16, 128:]
            return 0

        with jax.named_scope("wo"):
            lax.fori_loop(0, 4, columns, 0)

    def sequences(it, _):
        with jax.named_scope("attend"):
            attend(it)

        @pl.when((lax.rem(it, 2) == 1) & (it >= 8))
        def _():
            start_mlp4(2 * (it - 1 - 8))

        @pl.when(it == 7)
        def _():
            wo_pass(0, 32)

        @pl.when((it == 11) | (it == 15))
        def _():
            wo_pass((it - 3) * 4, 16)

        @pl.when((lax.rem(it, 2) == 1) & (it >= 7))
        def _():
            tick1((it - 7) // 2)
        return 0

    lax.fori_loop(0, 16, sequences, 0)
    start_mlp4(16)
    start_mlp4(20)

    def rest1(t, _):
        tick1(t)
        return 0

    lax.fori_loop(5, 5 + LAST, rest1, 0)

    def gate_up(cb, _):
        m = 4 * cb
        outs = []
        for r in range(4):
            ready(mlp_slot(m + r))
        for r in range(2):
            s0, s1 = mlp_slot(m + 2 * r), mlp_slot(m + 2 * r + 1)
            acc = jnp.dot(ab[:, pl.ds(0, DEEP)], ring[s0], preferred_element_type=F32)
            outs.append(acc + jnp.dot(ab[:, pl.ds(DEEP, DEEP)], ring[s1], preferred_element_type=F32))
        hidden[:, pl.ds(mult(cb * WIDE, WIDE), WIDE)] = (jax.nn.silu(outs[0]) * outs[1]).astype(BF16)
        start_mlp4(m + SLOTS)
        return 0

    with jax.named_scope("gate_up"):
        lax.fori_loop(0, up_blocks, gate_up, 0)

    def residual2(g):
        pieces = [states[pl.ds(mult(c * 1024 + g * 128 + me * 16, 16), 16), :] for c in range(chunks)]
        return jnp.concatenate(pieces, 0).astype(F32)

    groups = d // 1024

    def done2(g):
        for o in range(n):
            p = g * n + o
            pltpu.make_async_copy(y.at[pl.ds(mult(p * rows, rows), rows)], out.at[:, pl.ds(mult(p * 128, 128), 128)], out_sem.at[g]).start()

    second = functools.partial(steps, piece_rows=rows, box=box2, stage=stage2, send=send2, recv=recv2,
                               whole=y, residual=residual2, done=done2)

    def down(t, _):
        @pl.when(t < groups)
        def _():
            with jax.named_scope("down"):
                for i in range(4):
                    ready(mlp_slot(4 * up_blocks + 4 * t + i), down_rows)
                for i in range(4):
                    nb = 4 * t + i
                    slot = mlp_slot(4 * up_blocks + nb)
                    acc = jnp.dot(hidden[...], ring[slot, pl.ds(0, down_rows)], preferred_element_type=F32)
                    part[pl.ds(mult(nb * 2 * rows, rows), rows), :] = acc[:, :128]
                    part[pl.ds(mult(nb * 2 * rows + rows, rows), rows), :] = acc[:, 128:]
            start_mlp4(4 * up_blocks + 4 * t + SLOTS)

        for s in [0] + list(range(LAST, 0, -1)):
            @pl.when((t >= 2 * s) & (t - 2 * s < groups))
            def _():
                with jax.named_scope(f"b{s}"):
                    second(s, t - 2 * s)
        return 0

    lax.fori_loop(0, groups + 2 * LAST, down, 0)
    first(LAST + 1, chunks - 1)
    second(LAST + 1, groups - 1)
    for g in range(groups):
        piece = y.at[pl.ds(0, n * rows)]
        pltpu.make_async_copy(piece, piece, out_sem.at[g]).wait()


def solution(mesh):
    n = mesh.shape["tp"]

    def step(x, k_cache, v_cache, gain_a, wq, wo, gain_m, w_gate, w_up, w_down):
        rows, d = x.shape
        batch, keys, _, head = k_cache.shape
        ff = w_gate.shape[1]
        half = head // 2
        angle = np.float32(keys - 1) * THETA ** (-np.arange(half) / half)
        cos, sin = np.cos(angle), np.sin(angle)
        trig = jnp.asarray(np.stack([np.concatenate([cos, cos]), np.concatenate([-sin, sin])]), F32)
        any_ = pl.BlockSpec(memory_space=pl.ANY)
        chunks, groups = rows // 16, d // 1024
        dma = pltpu.SemaphoreType.DMA
        out = pl.pallas_call(
            functools.partial(layer, n),
            out_shape=jax.ShapeDtypeStruct((rows, d), BF16),
            in_specs=[any_] * 11,
            out_specs=any_,
            scratch_shapes=[
                pltpu.VMEM((SLOTS, DEEP, WIDE), BF16),
                pltpu.VMEM((rows, d), BF16),
                pltpu.VMEM((rows, d), BF16),
                pltpu.VMEM((rows * d // 128, 128), BF16),
                pltpu.VMEM((rows * d // 128, 128), BF16),
                pltpu.VMEM((rows * d // 128, 128), F32),
                pltpu.VMEM((rows, ff), BF16),
                pltpu.VMEM((rows * 8, head), F32),
                pltpu.VMEM((rows * 8, head), F32),
                pltpu.VMEM((d // 128, 128), BF16),
                pltpu.VMEM((d // 128, 128), BF16),
                pltpu.VMEM((2, 128), F32),
                pltpu.VMEM((chunks, 7, 128, 128), BF16),
                pltpu.VMEM((groups, 7, rows, 128), BF16),
                pltpu.VMEM((7, 128, 128), BF16),
                pltpu.VMEM((7, rows, 128), BF16),
                dma((SLOTS,)),
                dma((4,)),
                dma((groups,)),
                dma((14,)),
                dma((14,)),
                dma((chunks, 14)),
                dma((groups, 14)),
            ],
            compiler_params=pltpu.CompilerParams(collective_id=0, has_side_effects=True, vmem_limit_bytes=67043328),
            name="decoder_layer",
        )(x, k_cache.reshape(batch, keys, head), v_cache.reshape(batch, keys, head), gain_a.reshape(d // 128, 128), wq, wo,
          gain_m.reshape(d // 128, 128), w_gate, w_up, w_down, trig)
        return out

    states, cache, columns, rows_of = P("dp", None), P("dp", None, "tp", None), P(None, "tp"), P("tp", None)
    return jax.shard_map(
        step,
        mesh=mesh,
        in_specs=(states, cache, cache, P(None), columns, rows_of, P(None), columns, columns, rows_of),
        out_specs=states,
        check_vma=False,
    )
```

time: 191 us -> 148 us (0.77)
  Pallas kernels: 184 us -> 145 us
  other arithmetic: 3.99 us -> 0 us
    pallas_call x1, Pallas kernels: 184 us -> 145 us  [step(): pl.pallas_call(functools.partial(layer, n), out_shape=jax.ShapeDtypeStruc...]
    broadcast_in_dim x2 -> x0, other arithmetic: 2.67 us -> none  [the longest x1 1.33 us: step(): gain_m.astype(F32)[None]]
    reshape x1 -> x0, local copies, waits for them, and re-layouts: 2.39 us -> none  [step(): return out.reshape(d // 128, rows, 128).transpose(1, 0, 2).reshape(rows, d)]
    unnamed x0 -> x1, local copies, waits for them, and re-layouts: none -> 2.26 us
where the time goes in v2:
time: 148 us
  Pallas kernels  145 us (98%)
  local copies, waits for them, and re-layouts  2.26 us (2%)
    pallas_call x1, Pallas kernels, step(): pl.pallas_call(functools.partial(layer, n), out_shape=jax.ShapeDtypeStruc...  145 us

profile of v2, /device:TPU:30, one launch (start us, length us, event | category | flops | bytes accessed | tf_op | source)
XLA Modules:
  0.0 147.5 jit_solution(15942942286256605776)
XLA Ops:
  0.0 145.3 %decoder_layer.1 = bf16[64,8192]{1,0:T(8,128)(2,1)} custom-call(bf16[64,8192]{1,0:T(8,128)(2,1)} %x_hbm.1, bf16[64,2048,128]{2,1,0:T(8,128)(2,1)} %bitcast.4, bf16[64,2048,128]{2,1,0:T(8,128)(2,1)} %bitcast.5, bf16[64,128]{1,0:T(8,128)(2,1)} %bitcast.6, bf16[8192,1024]{1,0:T(8,128)(2,1)} %wq.1, bf16[1024,8192]{1,0:T(8,128)(2,1)} %wo.1, ...), custom_call_target="tpu_custom_call" | custom-call | tf_op jit(solution)/shard_map/decoder_layer/pallas_call | solution.py:396
  145.3 2.3 %copy.13 = bf16[64,8192]{1,0:T(8,128)(2,1)} copy(bf16[64,8192]{1,0:T(8,128)(2,1)} %decoder_layer.1) | data formatting | bytes 2097152

commit v3 on v2

--- a/solution.py
+++ b/solution.py
@@ -14,6 +14,7 @@
 
 DEEP, WIDE = 4096, 256
 SLOTS = 24
+LIMIT = 62 * 2**20
 HELD = 8
 
 
@@ -21,9 +22,9 @@
     return pl.multiple_of(v, k)
 
 
-def layer(n, x_hbm, kc, vc, gain_a_hbm, wq, wo, gain_m_hbm, wg, wu, wd, trig_hbm, out,
-          ring, x, ab, states, y, part, hidden, q3, seen3, gain_a, gain_m, trig, box1, box2, stage1, stage2,
-          slot_sem, x_sem, out_sem, send1, send2, recv1, recv2):
+def layer(n, x_hbm, kc, vc, gain_a_hbm, wq, wo, gain_m_hbm, wg, wu, wd, trig_hbm, y,
+          ring, x, ab, states, part, hidden, q3, seen3, gain_a, gain_m, trig, box1, box2, stage1, stage2,
+          slot_sem, x_sem, send1, send2, recv1, recv2):
     me = lax.axis_index("tp")
     rows, d = x_hbm.shape
     head = kc.shape[2]
@@ -99,75 +100,57 @@
             return pl.ds(mult((g * n + o) * piece_rows, piece_rows), piece_rows)
 
         def remote(i, src, dst, to):
-            return pltpu.make_async_remote_copy(src_ref=src, dst_ref=dst, send_sem=send.at[i], recv_sem=recv.at[g, i],
+            return pltpu.make_async_remote_copy(src_ref=src, dst_ref=dst, send_sem=send.at[g, i], recv_sem=recv.at[g, i],
                                                 device_id={"tp": dev(to)}, device_id_type=pl.DeviceIdType.MESH)
 
         def term(i, to):
-            return remote(i, stage.at[i], box.at[g, i], to)
+            return remote(i, stage.at[g, i], box.at[g, i], to)
 
         def piece(i, owner, to):
             ref = whole.at[at(dev(owner))]
             return remote(7 + i, ref, ref, to)
-
-        def go(copy):
-            @pl.when(g > 0)
-            def _():
-                copy.wait_send()
-
-            copy.start()
 
         def send_term(i, owner, to, *terms):
             value = part[at(dev(owner)), :]
             for k in terms:
                 term(k, 0).wait_recv()
                 value = value + box[g, k].astype(F32)
-            copy = term(i, to)
-
-            @pl.when(g > 0)
-            def _():
-                copy.wait_send()
-
-            stage[i] = value.astype(BF16)
-            copy.start()
-
-        def forward(k, i, owner, to):
-            piece(k, owner, 0).wait_recv()
-            go(piece(i, owner, to))
+            stage[g, i] = value.astype(BF16)
+            term(i, to).start()
 
         if s == 0:
-            send_term(0, 4, 1)
-            send_term(2, -3, -1)
-            send_term(1, 1, 1)
+            send_term(0, 4, 2)
+            send_term(1, 3, 1)
+            send_term(3, -3, -1)
+            send_term(2, 1, 1)
+            send_term(4, -1, -1)
         if s == 1:
-            send_term(3, 3, 1, 0)
-            send_term(4, -2, -1, 2)
+            send_term(6, -2, -2, 3)
+            send_term(5, 2, 2, 1, 0)
         if s == 2:
-            send_term(5, 2, 2, 3)
-            send_term(6, -1, -1, 4)
-        if s == 3:
             value = part[at(me), :]
-            for k in (1, 5, 6):
+            for k in (2, 4, 6, 5):
                 term(k, 0).wait_recv()
                 value = value + box[g, k].astype(F32)
             whole[at(me), :] = (residual(g) + value).astype(BF16)
-            for i, to in ((1, 2), (2, -1), (0, 1)):
-                go(piece(i, 0, to))
+            for i, to in ((0, 2), (2, -2), (1, 1), (3, -1)):
+                piece(i, 0, to).start()
+        if s == 3:
+            piece(2, 2, 0).wait_recv()
+            piece(6, 2, -1).start()
+            piece(0, -2, 0).wait_recv()
+            piece(4, -2, 2).start()
+            piece(5, -2, 1).start()
         if s == 4:
-            forward(1, 3, -2, 1)
-            forward(2, 4, 1, -1)
-        if s == 5:
-            forward(3, 5, -3, 1)
-            forward(4, 6, 2, -1)
-        if s == 6:
-            for i, owner in ((0, -1), (5, -4), (6, 3)):
+            for i, owner in ((1, -1), (3, 1), (4, -4), (5, -3), (6, 3)):
                 piece(i, owner, 0).wait_recv()
             done(g)
-        if s == 7:
+        if s == 5:
             for i in range(7):
                 term(i, 1).wait_send()
                 piece(i, 0, 1).wait_send()
 
-    LAST = 6
+    LAST = 4
 
     blocks = d // 128
 
@@ -231,16 +214,6 @@
 
     first = functools.partial(steps, piece_rows=chunk_rows * 8, box=box1, stage=stage1, send=send1, recv=recv1,
                               whole=states, residual=residual1, done=done1)
-
-    def tick1(t):
-        for s in [0] + list(range(1, LAST + 1)):
-            since = t - s
-
-            @pl.when((since == 0) | (since == 2) | (since == 4))
-            def _():
-                with jax.named_scope(f"a{s}"):
-                    begin = jnp.where(since == 0, 0, 1 + since // 2)
-                    lax.fori_loop(begin, 2 + since // 2, lambda g, _: (first(s, g), 0)[1], 0)
 
     def attend(it):
         ks, vs = kv_slot(2 * it), kv_slot(2 * it + 1)
@@ -297,28 +270,35 @@
         def _():
             start_mlp4(2 * (it - 1 - 8))
 
-        @pl.when(it == 7)
+        @pl.when(it == 9)
         def _():
             wo_pass(0, 32)
-
-        @pl.when((it == 11) | (it == 15))
-        def _():
-            wo_pass((it - 3) * 4, 16)
-
-        @pl.when((lax.rem(it, 2) == 1) & (it >= 7))
-        def _():
-            tick1((it - 7) // 2)
+            lax.fori_loop(0, 2, run1(0), 0)
+
+        @pl.when(it == 13)
+        def _():
+            lax.fori_loop(0, 2, run1(1), 0)
+
+        @pl.when((it == 12) | (it == 15))
+        def _():
+            c = (it - 6) // 3
+            wo_pass(c * 16, 16)
+            run1(0)(c, 0)
         return 0
+
+    def run1(s):
+        def body(g, _):
+            with jax.named_scope(f"a{s}"):
+                first(s, g)
+            return 0
+        return body
 
     lax.fori_loop(0, 16, sequences, 0)
     start_mlp4(16)
     start_mlp4(20)
 
-    def rest1(t, _):
-        tick1(t)
-        return 0
-
-    lax.fori_loop(5, 5 + LAST, rest1, 0)
+    for s, lo, hi in ((1, 2, 3), (2, 0, 2), (1, 3, 4), (2, 2, 3), (3, 0, 2), (2, 3, 4), (3, 2, 3), (4, 0, 2), (3, 3, 4), (4, 2, 4)):
+        lax.fori_loop(lo, hi, run1(s), 0)
 
     def gate_up(cb, _):
         m = 4 * cb
@@ -342,41 +322,50 @@
 
     groups = d // 1024
 
-    def done2(g):
-        for o in range(n):
-            p = g * n + o
-            pltpu.make_async_copy(y.at[pl.ds(mult(p * rows, rows), rows)], out.at[:, pl.ds(mult(p * 128, 128), 128)], out_sem.at[g]).start()
-
     second = functools.partial(steps, piece_rows=rows, box=box2, stage=stage2, send=send2, recv=recv2,
-                               whole=y, residual=residual2, done=done2)
+                               whole=y, residual=residual2, done=lambda g: None)
+
+    def run2(s):
+        def body(g, _):
+            with jax.named_scope(f"b{s}"):
+                second(s, g)
+            return 0
+        return body
 
     def down(t, _):
-        @pl.when(t < groups)
-        def _():
-            with jax.named_scope("down"):
-                for i in range(4):
-                    ready(mlp_slot(4 * up_blocks + 4 * t + i), down_rows)
-                for i in range(4):
-                    nb = 4 * t + i
-                    slot = mlp_slot(4 * up_blocks + nb)
-                    acc = jnp.dot(hidden[...], ring[slot, pl.ds(0, down_rows)], preferred_element_type=F32)
-                    part[pl.ds(mult(nb * 2 * rows, rows), rows), :] = acc[:, :128]
-                    part[pl.ds(mult(nb * 2 * rows + rows, rows), rows), :] = acc[:, 128:]
-            start_mlp4(4 * up_blocks + 4 * t + SLOTS)
-
-        for s in [0] + list(range(LAST, 0, -1)):
-            @pl.when((t >= 2 * s) & (t - 2 * s < groups))
+        with jax.named_scope("down"):
+            for i in range(4):
+                ready(mlp_slot(4 * up_blocks + 4 * t + i), down_rows)
+            for i in range(4):
+                nb = 4 * t + i
+                slot = mlp_slot(4 * up_blocks + nb)
+                acc = jnp.dot(hidden[...], ring[slot, pl.ds(0, down_rows)], preferred_element_type=F32)
+                part[pl.ds(mult(nb * 2 * rows, rows), rows), :] = acc[:, :128]
+                part[pl.ds(mult(nb * 2 * rows + rows, rows), rows), :] = acc[:, 128:]
+        start_mlp4(4 * up_blocks + 4 * t + SLOTS)
+        for s, lag in enumerate(LAGS):
+            @pl.when(t >= lag)
             def _():
-                with jax.named_scope(f"b{s}"):
-                    second(s, t - 2 * s)
+                run2(s)(t - lag, 0)
         return 0
 
-    lax.fori_loop(0, groups + 2 * LAST, down, 0)
-    first(LAST + 1, chunks - 1)
-    second(LAST + 1, groups - 1)
-    for g in range(groups):
-        piece = y.at[pl.ds(0, n * rows)]
-        pltpu.make_async_copy(piece, piece, out_sem.at[g]).wait()
+    LAGS = (0, 2, 5, 7)
+    lax.fori_loop(0, groups, down, 0)
+    for s, g in ((2, 3), (3, 1), (2, 4), (1, 6), (3, 2), (1, 7), (2, 5), (3, 3), (2, 6), (3, 4), (2, 7), (3, 5), (3, 6), (3, 7)):
+        run2(s)(jnp.int32(g), 0)
+    lax.fori_loop(0, groups, run2(LAST), 0)
+    lax.fori_loop(0, chunks, lambda g, _: (first(LAST + 1, g), 0)[1], 0)
+    lax.fori_loop(0, groups, lambda g, _: (second(LAST + 1, g), 0)[1], 0)
+
+
+def place(y, out, sem):
+    rows, d = out.shape
+
+    def copy(p):
+        return pltpu.make_async_copy(y.at[pl.ds(mult(p * rows, rows), rows)], out.at[:, pl.ds(mult(p * 128, 128), 128)], sem)
+
+    lax.fori_loop(0, d // 128, lambda p, _: (copy(p).start(), 0)[1], 0)
+    pltpu.make_async_copy(y, y, sem).wait()
 
 
 def solution(mesh):
@@ -393,16 +382,15 @@
         any_ = pl.BlockSpec(memory_space=pl.ANY)
         chunks, groups = rows // 16, d // 1024
         dma = pltpu.SemaphoreType.DMA
-        out = pl.pallas_call(
+        pieces = pl.pallas_call(
             functools.partial(layer, n),
-            out_shape=jax.ShapeDtypeStruct((rows, d), BF16),
+            out_shape=pltpu.VMEM((rows * d // 128, 128), BF16),
             in_specs=[any_] * 11,
-            out_specs=any_,
+            out_specs=pl.BlockSpec(memory_space=pltpu.VMEM),
             scratch_shapes=[
                 pltpu.VMEM((SLOTS, DEEP, WIDE), BF16),
                 pltpu.VMEM((rows, d), BF16),
                 pltpu.VMEM((rows, d), BF16),
-                pltpu.VMEM((rows * d // 128, 128), BF16),
                 pltpu.VMEM((rows * d // 128, 128), BF16),
                 pltpu.VMEM((rows * d // 128, 128), F32),
                 pltpu.VMEM((rows, ff), BF16),
@@ -413,21 +401,28 @@
                 pltpu.VMEM((2, 128), F32),
                 pltpu.VMEM((chunks, 7, 128, 128), BF16),
                 pltpu.VMEM((groups, 7, rows, 128), BF16),
-                pltpu.VMEM((7, 128, 128), BF16),
-                pltpu.VMEM((7, rows, 128), BF16),
+                pltpu.VMEM((chunks, 7, 128, 128), BF16),
+                pltpu.VMEM((groups, 7, rows, 128), BF16),
                 dma((SLOTS,)),
                 dma((4,)),
-                dma((groups,)),
-                dma((14,)),
-                dma((14,)),
+                dma((chunks, 14)),
+                dma((groups, 14)),
                 dma((chunks, 14)),
                 dma((groups, 14)),
             ],
-            compiler_params=pltpu.CompilerParams(collective_id=0, has_side_effects=True, vmem_limit_bytes=67043328),
+            compiler_params=pltpu.CompilerParams(collective_id=0, has_side_effects=True, vmem_limit_bytes=LIMIT),
             name="decoder_layer",
         )(x, k_cache.reshape(batch, keys, head), v_cache.reshape(batch, keys, head), gain_a.reshape(d // 128, 128), wq, wo,
           gain_m.reshape(d // 128, 128), w_gate, w_up, w_down, trig)
-        return out
+        return pl.pallas_call(
+            place,
+            out_shape=jax.ShapeDtypeStruct((rows, d), BF16),
+            in_specs=[pl.BlockSpec(memory_space=pltpu.VMEM)],
+            out_specs=any_,
+            scratch_shapes=[dma(())],
+            compiler_params=pltpu.CompilerParams(vmem_limit_bytes=2**22),
+            name="place",
+        )(pieces)
 
     states, cache, columns, rows_of = P("dp", None), P("dp", None, "tp", None), P(None, "tp"), P("tp", None)
     return jax.shard_map(

time: 148 us -> 136 us (0.919)
  Pallas kernels: 145 us -> 136 us
  local copies, waits for them, and re-layouts: 2.26 us -> 0 us
    pallas_call x1 -> x2, Pallas kernels: 145 us -> 136 us  [the longest x1 135 us: step(): pl.pallas_call(functools.partial(layer, n), out_shape=pltpu.VMEM((rows *...]
    unnamed x1 -> x0, local copies, waits for them, and re-layouts: 2.26 us -> none
where the time goes in v3:
time: 136 us
  Pallas kernels  136 us (100%)
    pallas_call x1, Pallas kernels, step(): pl.pallas_call(functools.partial(layer, n), out_shape=pltpu.VMEM((rows *...  135 us

profile of v3, /device:TPU:30, one launch (start us, length us, event | category | flops | bytes accessed | tf_op | source)
XLA Modules:
  0.0 136.0 jit_solution(75059598841593236)
XLA Ops:
  0.0 134.8 %decoder_layer.1.y = bf16[4096,128]{1,0:T(8,128)(2,1)S(1)} custom-call(bf16[64,8192]{1,0:T(8,128)(2,1)} %x_hbm.1, bf16[64,2048,128]{2,1,0:T(8,128)(2,1)} %bitcast.4, bf16[64,2048,128]{2,1,0:T(8,128)(2,1)} %bitcast.5, bf16[64,128]{1,0:T(8,128)(2,1)} %bitcast.6, bf16[8192,1024]{1,0:T(8,128)(2,1)} %wq.1, bf16[1024,8192]{1,0:T(8,128)(2,1)} %wo.1, ...), custom_call_target="tpu_custom_call" | custom-call | tf_op jit(solution)/shard_map/decoder_layer/pallas_call | solution.py:385
  134.8 1.2 place.1

commit v4 on v3

--- a/solution.py
+++ b/solution.py
@@ -349,13 +349,14 @@
                 run2(s)(t - lag, 0)
         return 0
 
-    LAGS = (0, 2, 5, 7)
+    LAGS = (0, 2, 4, 7)
     lax.fori_loop(0, groups, down, 0)
-    for s, g in ((2, 3), (3, 1), (2, 4), (1, 6), (3, 2), (1, 7), (2, 5), (3, 3), (2, 6), (3, 4), (2, 7), (3, 5), (3, 6), (3, 7)):
+    for s, g in ((1, 6), (3, 1), (2, 4), (1, 7), (3, 2), (2, 5), (3, 3), (2, 6), (3, 4), (2, 7), (3, 5), (3, 6), (3, 7)):
         run2(s)(jnp.int32(g), 0)
+    lax.fori_loop(0, chunks, run1(LAST + 1), 0)
+    lax.fori_loop(0, groups - 2, run2(LAST + 1), 0)
     lax.fori_loop(0, groups, run2(LAST), 0)
-    lax.fori_loop(0, chunks, lambda g, _: (first(LAST + 1, g), 0)[1], 0)
-    lax.fori_loop(0, groups, lambda g, _: (second(LAST + 1, g), 0)[1], 0)
+    lax.fori_loop(groups - 2, groups, run2(LAST + 1), 0)
 
 
 def place(y, out, sem):

time: 136 us -> 135 us (level)
  no operation moved by 1% of the time
where the time goes in v4:
time: 135 us
  Pallas kernels  135 us (100%)
    pallas_call x1, Pallas kernels, step(): pl.pallas_call(functools.partial(layer, n), out_shape=pltpu.VMEM((rows *...  134 us

profile of v4, /device:TPU:30, one launch (start us, length us, event | category | flops | bytes accessed | tf_op | source)
XLA Modules:
  0.0 134.9 jit_solution(6594832340992309087)
XLA Ops:
  0.0 133.7 %decoder_layer.1.y = bf16[4096,128]{1,0:T(8,128)(2,1)S(1)} custom-call(bf16[64,8192]{1,0:T(8,128)(2,1)} %x_hbm.1, bf16[64,2048,128]{2,1,0:T(8,128)(2,1)} %bitcast.4, bf16[64,2048,128]{2,1,0:T(8,128)(2,1)} %bitcast.5, bf16[64,128]{1,0:T(8,128)(2,1)} %bitcast.6, bf16[8192,1024]{1,0:T(8,128)(2,1)} %wq.1, bf16[1024,8192]{1,0:T(8,128)(2,1)} %wo.1, ...), custom_call_target="tpu_custom_call" | custom-call | tf_op jit(solution)/shard_map/decoder_layer/pallas_call | solution.py:386
  133.7 1.2 place.1
